TPU v7x, 32 devices: a whole 2x2x4 slice. The times are simulated.
32 devices in a mesh: hi: 4 (over y, core), lo: 8 (over z, x).
Axes of the slice: x: 2, y: 2, z: 4, core: 2. Of those that a mesh axis runs over, the one named last changes fastest.
Arguments:
- grm: bfloat16 [4, 8, 64, 4, 512], P(None, 'lo', None, 'hi'), as said below
- right_sides: float32 [2048, 512], P(('hi', 'lo')), may hold values from -6 to 6
- inv_diag: float32 [2048], P(('hi', 'lo')), may hold values from 0.3 to 1
- bases: float32 [2048, 576], P(('hi', 'lo')), may hold values from -0.75 to 0.75
- couplings: float32 [9, 64, 64], replicated, as said below
- level_map: int32 [8], replicated, may hold values from 0 to 7, each once
- variance: float32 [2], replicated, may hold values from 0.3 to 1.5
- iters_per_column: int32 [512], replicated, may hold values from 1 to 3
Outputs:
- solution: float32 [2048, 512], P(('hi', 'lo'))
- residual: float32 [2048, 512], P(('hi', 'lo'))
Inputs may be any that keep to these rules, and one draw needn't show every extreme that they name: `grm`: G is symmetric and positive definite. `couplings`: each of the 9 matrices is symmetric and positive definite. `level_map`: a permutation of the levels.
All inputs are finite; a program needn't handle non-finite values.
Results may differ from a plain program's by a relative error of at most 0.0055.
Values may be sent and summed in bfloat16 or wider, within the bound.
A program may use at most 64 MiB of HBM per device.

v0:
```python
import jax
import jax.numpy as jnp
from jax import lax
from jax.sharding import PartitionSpec as P

ITERS = 3


def from_partner(value, axis, bit):
    mask = 2**bit
    pairs = [(source, source ^ mask) for source in range(lax.axis_size(axis))]
    return lax.ppermute(value, axis, pairs)


def level_pieces(coefficients, couplings, level):
    level_ids = jnp.arange(couplings.shape[0], dtype=jnp.int32)
    select = (level_ids == level).astype(jnp.float32)
    own_part = jnp.einsum("l,lrb->rb", select, coefficients)
    matrix = jnp.einsum("l,lrs->rs", select, couplings)
    return (own_part, matrix, select)


def add_level(stacked, own_part, other_part, matrix, select):
    term = jnp.dot(matrix, own_part + other_part, precision=lax.Precision.HIGHEST)
    return stacked + select[:, None, None] * term[None]


def local(grm, right_sides, inv_diag, bases, couplings, level_map, variance, iters_per_column):
    row_count, column_count = right_sides.shape
    grm_block = grm.reshape(-1, grm.shape[4])
    level_total = couplings.shape[0]
    rank_width = couplings.shape[1]
    lo_bits = lax.axis_size("lo").bit_length() - 1
    hi_bits = lax.axis_size("hi").bit_length() - 1
    genetic = variance[0]
    noise = variance[1]

    def precondition(resid):
        coefficients = lax.dot_general(
            bases, resid, (((0,), (0,)), ((), ())), precision=lax.Precision.HIGHEST
        )
        coefficients = coefficients.reshape(level_total, rank_width, column_count)
        stacked = jnp.zeros((level_total - 1, rank_width, column_count), jnp.float32)
        for bit_index in range(lo_bits):
            own_part, matrix, select = level_pieces(coefficients, couplings, level_map[bit_index])
            other_part = from_partner(own_part.astype(jnp.bfloat16), "lo", bit_index).astype(
                own_part.dtype
            )
            stacked = add_level(stacked, own_part, other_part, matrix, select[: level_total - 1])
        for bit_index in range(hi_bits):
            own_part, matrix, select = level_pieces(
                coefficients, couplings, level_map[lo_bits + bit_index]
            )
            other_part = from_partner(own_part.astype(jnp.bfloat16), "hi", bit_index).astype(
                own_part.dtype
            )
            stacked = add_level(stacked, own_part, other_part, matrix, select[: level_total - 1])
        split_at = (level_total - 1) * rank_width
        local_part = inv_diag[:, None] * resid + jnp.dot(
            bases[:, :split_at],
            stacked.reshape(split_at, column_count),
            precision=lax.Precision.HIGHEST,
        )
        coarse_basis = bases[:, split_at:]
        partial_energy = jnp.sum(resid * local_part, axis=0)
        total, summed_energy = lax.psum(
            (coefficients[level_total - 1], partial_energy), ("hi", "lo")
        )
        coarse = jnp.dot(couplings[level_total - 1], total, precision=lax.Precision.HIGHEST)
        scaled = local_part + jnp.dot(coarse_basis, coarse, precision=lax.Precision.HIGHEST)
        energy = summed_energy + jnp.sum(total * coarse, axis=0)
        return (scaled, energy)

    solution = jnp.zeros_like(right_sides)
    residual = right_sides
    scaled, energy = precondition(residual)
    direction = scaled
    for step in range(ITERS):
        rounded = direction.astype(jnp.bfloat16)
        partial_value = jnp.dot(
            grm_block,
            lax.all_gather(rounded, "lo", axis=0, tiled=True),
            preferred_element_type=jnp.float32,
        )
        product = lax.psum_scatter(partial_value, "hi", scatter_dimension=0, tiled=True)
        image = genetic * product + noise * direction
        curvature = lax.psum(jnp.sum(direction * image, axis=0), ("hi", "lo"))
        alpha = energy / curvature
        stepsize = jnp.where(step < iters_per_column, alpha, jnp.zeros_like(alpha))
        solution = solution + stepsize * direction
        residual = residual - stepsize * image
        if step + 1 < ITERS:
            scaled, fresh = precondition(residual)
            direction = scaled + fresh / energy * direction
            energy = fresh
    return (solution, residual)


def solution(mesh):
    in_specs = (
        P(None, "lo", None, "hi", None),
        P(("hi", "lo"), None),
        P(("hi", "lo")),
        P(("hi", "lo"), None),
        P(),
        P(),
        P(),
        P(),
    )
    out_specs = (P(("hi", "lo"), None), P(("hi", "lo"), None))
    return jax.shard_map(local, mesh=mesh, in_specs=in_specs, out_specs=out_specs, check_vma=False)
```

profile of v0, /device:TPU:0, one launch (start us, length us, event | category | flops | bytes accessed | tf_op | source)
XLA Modules:
  0.0 806.3 jit_solution(18174941709177877963)
XLA Ops:
  7.2 1.5 fusion.146
  8.7 2.1 fusion.150
  10.8 1.3 fusion.26
  12.1 3.1 collective-permute-start.1
  15.3 1.4 fusion.24
  16.6 2.7 collective-permute-start.2
  19.3 1.4 fusion.22
  20.8 1.4 fusion.20
  22.1 1.6 collective-permute-start.4
  23.7 1.4 fusion.28
  25.1 1.6 collective-permute-start
  30.6 0.9 fusion.58
  31.5 0.9 fusion.54
  32.4 0.8 fusion.56
  33.3 0.9 fusion.50
  34.2 0.9 fusion.52
  35.8 112.5 %all-reduce.5.cloned.1.call-done = f32[64,512]{1,0:T(8,128)} async-done(((f32[64,512]{1,0:T(8,128)}), f32[64,512]{1,0:T(8,128)}) %all-reduce.5.cloned.1.call-update) | async-done | bytes 131088 | tf_op jit(solution)/shard_map/psum | solution.py:66
  148.4 1.3 fusion.72
  151.6 0.8 multiply_reduce_fusion.5
  152.7 31.3 %all_gather.9 = bf16[512,512]{1,0:T(8,128)(2,1)S(1)} all-gather(bf16[64,512]{1,0:T(8,128)(2,1)S(1)} %get-tuple-element.19), channel_id=1, replica_groups=mesh['hi'=4,'lo'=8] {'lo'}, dimensions={0}, use_global_device_ids=true | all-gather | bytes 589824 | tf_op jit(solution)/shard_map/all_gather | solution.py:82
  184.0 1.1 convolution_bitcast_fusion.2
  185.8 20.3 %reduce-scatter.4.cloned.1.call-done = f32[64,512]{1,0:T(8,128)} async-done(((f32[256,512]{1,0:T(8,128)}), f32[64,512]{1,0:T(8,128)}) %reduce-scatter.4.cloned.1.call-update) | async-done | bytes 131088 | tf_op jit(solution)/shard_map/reduce_scatter | solution.py:85
  206.1 2.2 multiply_reduce_fusion.4
  208.3 39.5 %all-reduce = (f32[512]{0:T(512)S(1)}, f32[512]{0:T(512)S(1)}) all-reduce(f32[512]{0:T(512)S(1)} %get-tuple-element.21, f32[512]{0:T(512)S(1)} %multiply_reduce_fusion.4), channel_id=1, replica_groups=mesh['hi'=4,'lo'=8] {'hi','lo'}, use_global_device_ids=true, to_apply=%region_1.0 | all-reduce | flops 1024 | bytes 8192 | tf_op jit(solution)/shard_map/psum | solution.py:66
  247.8 2.2 multiply_subtract_fusion.2
  249.9 1.1 fusion.151
  251.1 1.3 fusion.16
  252.4 1.4 fusion.14
  253.8 1.4 fusion.12
  255.1 1.4 fusion.10
  257.2 1.4 fusion.18
  258.6 1.5 collective-permute-start.6
  260.2 1.4 collective-permute-start.7
  261.7 2.3 collective-permute-start.9
  264.1 1.6 collective-permute-start.5
  265.6 117.0 %all-reduce.7.cloned.1.call-done = f32[64,512]{1,0:T(8,128)} async-done(((f32[64,512]{1,0:T(8,128)}), f32[64,512]{1,0:T(8,128)}) %all-reduce.7.cloned.1.call-update) | async-done | bytes 131088 | tf_op jit(solution)/shard_map/psum | solution.py:66
  382.6 1.3 fusion.66
  386.6 39.3 %psum.66 = f32[512]{0:T(512)S(1)} all-reduce(f32[512]{0:T(512)S(1)} %get-tuple-element.25), channel_id=1, replica_groups=mesh['hi'=4,'lo'=8] {'hi','lo'}, use_global_device_ids=true, to_apply=%region_8.9 | all-reduce | flops 512 | bytes 4096 | tf_op jit(solution)/shard_map/psum | solution.py:66
  426.1 31.2 %all_gather.10 = bf16[512,512]{1,0:T(8,128)(2,1)S(1)} all-gather(bf16[64,512]{1,0:T(8,128)(2,1)S(1)} %get-tuple-element.29), channel_id=1, replica_groups=mesh['hi'=4,'lo'=8] {'lo'}, dimensions={0}, use_global_device_ids=true | all-gather | bytes 589824 | tf_op jit(solution)/shard_map/all_gather | solution.py:82
  457.3 1.1 convolution_bitcast_fusion.1
  458.5 22.0 %reduce-scatter.6.cloned.1.call-done = f32[64,512]{1,0:T(8,128)} async-done(((f32[256,512]{1,0:T(8,128)}), f32[64,512]{1,0:T(8,128)}) %reduce-scatter.6.cloned.1.call-update) | async-done | bytes 131088 | tf_op jit(solution)/shard_map/reduce_scatter | solution.py:85
  480.5 2.2 multiply_reduce_fusion.2
  482.7 39.5 %psum.68 = f32[512]{0:T(512)S(1)} all-reduce(f32[512]{0:T(512)S(1)} %multiply_reduce_fusion.2), channel_id=1, replica_groups=mesh['hi'=4,'lo'=8] {'hi','lo'}, use_global_device_ids=true, to_apply=%region_13.14 | all-reduce | flops 512 | bytes 4096 | tf_op jit(solution)/shard_map/psum | solution.py:87
  522.2 2.2 multiply_subtract_fusion.1
  524.4 1.1 fusion.152
  525.6 1.3 fusion.6
  526.9 1.4 fusion.4
  528.2 1.4 fusion.2
  529.6 1.4 fusion
  531.7 1.4 fusion.8
  533.1 1.5 collective-permute-start.11
  534.7 1.4 collective-permute-start.12
  536.2 2.3 collective-permute-start.14
  538.5 1.5 collective-permute-start.10
  540.1 117.0 %all-reduce.9.cloned.1.call-done = f32[64,512]{1,0:T(8,128)} async-done(((f32[64,512]{1,0:T(8,128)}), f32[64,512]{1,0:T(8,128)}) %all-reduce.9.cloned.1.call-update) | async-done | bytes 131088 | tf_op jit(solution)/shard_map/psum | solution.py:66
  657.1 1.3 fusion.60
  660.2 0.8 multiply_reduce_fusion.1
  661.0 39.3 %psum.69 = f32[512]{0:T(512)S(1)} all-reduce(f32[512]{0:T(512)S(1)} %get-tuple-element.31), channel_id=1, replica_groups=mesh['hi'=4,'lo'=8] {'hi','lo'}, use_global_device_ids=true, to_apply=%region_15.16 | all-reduce | flops 512 | bytes 4096 | tf_op jit(solution)/shard_map/psum | solution.py:66
  700.6 31.2 %all_gather.11 = bf16[512,512]{1,0:T(8,128)(2,1)S(1)} all-gather(bf16[64,512]{1,0:T(8,128)(2,1)S(1)} %get-tuple-element.35), channel_id=1, replica_groups=mesh['hi'=4,'lo'=8] {'lo'}, dimensions={0}, use_global_device_ids=true | all-gather | bytes 589824 | tf_op jit(solution)/shard_map/all_gather | solution.py:82
  731.8 1.1 convolution_bitcast_fusion
  732.9 22.1 %reduce-scatter.8.cloned.1.call-done = f32[64,512]{1,0:T(8,128)} async-done(((f32[256,512]{1,0:T(8,128)}), f32[64,512]{1,0:T(8,128)}) %reduce-scatter.8.cloned.1.call-update) | async-done | bytes 131088 | tf_op jit(solution)/shard_map/reduce_scatter | solution.py:85
  755.1 2.2 multiply_reduce_fusion
  757.2 39.3 %psum.71 = f32[512]{0:T(512)S(1)} all-reduce(f32[512]{0:T(512)S(1)} %multiply_reduce_fusion), channel_id=1, replica_groups=mesh['hi'=4,'lo'=8] {'hi','lo'}, use_global_device_ids=true, to_apply=%region_20.21 | all-reduce | flops 512 | bytes 4096 | tf_op jit(solution)/shard_map/psum | solution.py:87
  796.6 2.9 multiply_subtract_fusion
  (110 shorter events, 14.3 us)
Async XLA Ops:
  7.2 176.8 %copy-start = (bf16[4,1,64,1,512]{4,2,3,1,0:T(8,128)(2,1)S(1)}, bf16[4,1,64,1,512]{4,2,3,1,0:T(8,128)(2,1)}, u32[]{:S(2)}) copy-start(bf16[4,1,64,1,512]{4,2,3,1,0:T(8,128)(2,1)} %param.8) | copy-start | bytes 786436
  7.2 141.2 %all-reduce.5.cloned.1.call-start = ((), (), s32[]{:S(2)}) async-start(), calls=%async_computation.3 | async-start | bytes 262144 | tf_op jit(solution)/shard_map/psum | solution.py:66
  12.1 137.5 %collective-permute-start.1 = (bf16[64,512]{1,0:T(8,128)(2,1)S(1)}, bf16[64,512]{1,0:T(8,128)(2,1)S(1)}, u32[]{:S(2)}, u32[]{:S(2)}) collective-permute-start(bf16[64,512]{1,0:T(8,128)(2,1)S(1)} %bitcast.372), channel_id=1, source_target_pairs={{0,2},{1,3},{2,0},{3,1},{4,6},{5,7},{6,4},{7,5},{8,10},{9,11},{10,... | collective-permute-start | bytes 196616 | tf_op jit(solution)/shard_map/ppermute | solution.py:12
  16.6 133.3 %collective-permute-start.2 = (bf16[64,512]{1,0:T(8,128)(2,1)S(1)}, bf16[64,512]{1,0:T(8,128)(2,1)S(1)}, u32[]{:S(2)}, u32[]{:S(2)}) collective-permute-start(bf16[64,512]{1,0:T(8,128)(2,1)S(1)} %bitcast.371), channel_id=1, source_target_pairs={{0,4},{1,5},{2,6},{3,7},{4,0},{5,1},{6,2},{7,3},{8,12},{9,13},{10,... | collective-permute-start | bytes 196616 | tf_op jit(solution)/shard_map/ppermute | solution.py:12
  20.7 129.5 %collective-permute-start.3 = (bf16[64,512]{1,0:T(8,128)(2,1)S(1)}, bf16[64,512]{1,0:T(8,128)(2,1)S(1)}, u32[]{:S(2)}, u32[]{:S(2)}) collective-permute-start(bf16[64,512]{1,0:T(8,128)(2,1)S(1)} %bitcast.370), channel_id=1, source_target_pairs={{0,8},{8,0},{16,24},{24,16},{1,9},{9,1},{17,25},{25,17},{2,10},{10... | collective-permute-start | bytes 196616 | tf_op jit(solution)/shard_map/ppermute | solution.py:12
  22.1 8.5 %copy-start.1 = (f32[9,64,64]{2,1,0:T(8,128)S(1)}, f32[9,64,64]{2,1,0:T(8,128)}, u32[]{:S(2)}) copy-start(f32[9,64,64]{2,1,0:T(8,128)} %param.12) | copy-start | bytes 442372
  22.1 128.4 %collective-permute-start.4 = (bf16[64,512]{1,0:T(8,128)(2,1)S(1)}, bf16[64,512]{1,0:T(8,128)(2,1)S(1)}, u32[]{:S(2)}, u32[]{:S(2)}) collective-permute-start(bf16[64,512]{1,0:T(8,128)(2,1)S(1)} %bitcast.368), channel_id=1, source_target_pairs={{0,16},{8,24},{16,0},{24,8},{1,17},{9,25},{17,1},{25,9},{2,18},{10... | collective-permute-start | bytes 196616 | tf_op jit(solution)/shard_map/ppermute | solution.py:12
  25.1 125.7 %collective-permute-start = (bf16[64,512]{1,0:T(8,128)(2,1)S(1)}, bf16[64,512]{1,0:T(8,128)(2,1)S(1)}, u32[]{:S(2)}, u32[]{:S(2)}) collective-permute-start(bf16[64,512]{1,0:T(8,128)(2,1)S(1)} %bitcast.369), channel_id=1, source_target_pairs={{0,1},{1,0},{2,3},{3,2},{4,5},{5,4},{6,7},{7,6},{8,9},{9,8},{10,11... | collective-permute-start | bytes 196616 | tf_op jit(solution)/shard_map/ppermute | solution.py:12
  27.4 178.7 %reduce-scatter.4.cloned.1.call-start = ((), (), s32[]{:S(2)}) async-start(), calls=%async_computation.4 | async-start | bytes 655360 | tf_op jit(solution)/shard_map/reduce_scatter | solution.py:85
  150.5 1.1 copy-start.2
  150.5 1.0 copy-start.3
  150.5 1.0 copy-start.5
  152.7 32.5 %copy-start.6 = (f32[2]{0:T(128)S(1)}, f32[2]{0:T(128)}, u32[]{:S(2)}) copy-start(f32[2]{0:T(128)} %param.14) | copy-start | bytes 28
  184.0 63.8 %copy-start.4 = (s32[512]{0:T(512)S(1)}, s32[512]{0:T(512)}, u32[]{:S(2)}) copy-start(s32[512]{0:T(512)} %param.15) | copy-start | bytes 6148
  185.1 197.5 %all-reduce.7.cloned.1.call-start = ((), (), s32[]{:S(2)}) async-start(), calls=%async_computation.5 | async-start | bytes 262144 | tf_op jit(solution)/shard_map/psum | solution.py:66
  257.2 223.3 %reduce-scatter.6.cloned.1.call-start = ((), (), s32[]{:S(2)}) async-start(), calls=%async_computation.6 | async-start | bytes 655360 | tf_op jit(solution)/shard_map/reduce_scatter | solution.py:85
  258.6 125.2 %collective-permute-start.6 = (bf16[64,512]{1,0:T(8,128)(2,1)S(1)}, bf16[64,512]{1,0:T(8,128)(2,1)S(1)}, u32[]{:S(2)}, u32[]{:S(2)}) collective-permute-start(bf16[64,512]{1,0:T(8,128)(2,1)S(1)} %bitcast.381), channel_id=1, source_target_pairs={{0,2},{1,3},{2,0},{3,1},{4,6},{5,7},{6,4},{7,5},{8,10},{9,11},{10,... | collective-permute-start | bytes 196616 | tf_op jit(solution)/shard_map/ppermute | solution.py:12
  260.2 124.0 %collective-permute-start.7 = (bf16[64,512]{1,0:T(8,128)(2,1)S(1)}, bf16[64,512]{1,0:T(8,128)(2,1)S(1)}, u32[]{:S(2)}, u32[]{:S(2)}) collective-permute-start(bf16[64,512]{1,0:T(8,128)(2,1)S(1)} %bitcast.380), channel_id=1, source_target_pairs={{0,4},{1,5},{2,6},{3,7},{4,0},{5,1},{6,2},{7,3},{8,12},{9,13},{10,... | collective-permute-start | bytes 196616 | tf_op jit(solution)/shard_map/ppermute | solution.py:12
  261.6 122.8 %collective-permute-start.8 = (bf16[64,512]{1,0:T(8,128)(2,1)S(1)}, bf16[64,512]{1,0:T(8,128)(2,1)S(1)}, u32[]{:S(2)}, u32[]{:S(2)}) collective-permute-start(bf16[64,512]{1,0:T(8,128)(2,1)S(1)} %bitcast.378), channel_id=1, source_target_pairs={{0,8},{8,0},{16,24},{24,16},{1,9},{9,1},{17,25},{25,17},{2,10},{10... | collective-permute-start | bytes 196616 | tf_op jit(solution)/shard_map/ppermute | solution.py:12
  261.7 123.0 %collective-permute-start.9 = (bf16[64,512]{1,0:T(8,128)(2,1)S(1)}, bf16[64,512]{1,0:T(8,128)(2,1)S(1)}, u32[]{:S(2)}, u32[]{:S(2)}) collective-permute-start(bf16[64,512]{1,0:T(8,128)(2,1)S(1)} %bitcast.376), channel_id=1, source_target_pairs={{0,16},{8,24},{16,0},{24,8},{1,17},{9,25},{17,1},{25,9},{2,18},{10... | collective-permute-start | bytes 196616 | tf_op jit(solution)/shard_map/ppermute | solution.py:12
  264.1 121.0 %collective-permute-start.5 = (bf16[64,512]{1,0:T(8,128)(2,1)S(1)}, bf16[64,512]{1,0:T(8,128)(2,1)S(1)}, u32[]{:S(2)}, u32[]{:S(2)}) collective-permute-start(bf16[64,512]{1,0:T(8,128)(2,1)S(1)} %bitcast.375), channel_id=1, source_target_pairs={{0,1},{1,0},{2,3},{3,2},{4,5},{5,4},{6,7},{7,6},{8,9},{9,8},{10,11... | collective-permute-start | bytes 196616 | tf_op jit(solution)/shard_map/ppermute | solution.py:12
  458.4 198.6 %all-reduce.9.cloned.1.call-start = ((), (), s32[]{:S(2)}) async-start(), calls=%async_computation.7 | async-start | bytes 262144 | tf_op jit(solution)/shard_map/psum | solution.py:66
  531.7 223.4 %reduce-scatter.8.cloned.1.call-start = ((), (), s32[]{:S(2)}) async-start(), calls=%async_computation.8 | async-start | bytes 655360 | tf_op jit(solution)/shard_map/reduce_scatter | solution.py:85
  533.1 125.2 %collective-permute-start.11 = (bf16[64,512]{1,0:T(8,128)(2,1)S(1)}, bf16[64,512]{1,0:T(8,128)(2,1)S(1)}, u32[]{:S(2)}, u32[]{:S(2)}) collective-permute-start(bf16[64,512]{1,0:T(8,128)(2,1)S(1)} %bitcast.382), channel_id=1, source_target_pairs={{0,2},{1,3},{2,0},{3,1},{4,6},{5,7},{6,4},{7,5},{8,10},{9,11},{10,... | collective-permute-start | bytes 196616 | tf_op jit(solution)/shard_map/ppermute | solution.py:12
  534.7 124.0 %collective-permute-start.12 = (bf16[64,512]{1,0:T(8,128)(2,1)S(1)}, bf16[64,512]{1,0:T(8,128)(2,1)S(1)}, u32[]{:S(2)}, u32[]{:S(2)}) collective-permute-start(bf16[64,512]{1,0:T(8,128)(2,1)S(1)} %bitcast.379), channel_id=1, source_target_pairs={{0,4},{1,5},{2,6},{3,7},{4,0},{5,1},{6,2},{7,3},{8,12},{9,13},{10,... | collective-permute-start | bytes 196616 | tf_op jit(solution)/shard_map/ppermute | solution.py:12
  536.1 122.8 %collective-permute-start.13 = (bf16[64,512]{1,0:T(8,128)(2,1)S(1)}, bf16[64,512]{1,0:T(8,128)(2,1)S(1)}, u32[]{:S(2)}, u32[]{:S(2)}) collective-permute-start(bf16[64,512]{1,0:T(8,128)(2,1)S(1)} %bitcast.377), channel_id=1, source_target_pairs={{0,8},{8,0},{16,24},{24,16},{1,9},{9,1},{17,25},{25,17},{2,10},{10... | collective-permute-start | bytes 196616 | tf_op jit(solution)/shard_map/ppermute | solution.py:12
  536.2 123.0 %collective-permute-start.14 = (bf16[64,512]{1,0:T(8,128)(2,1)S(1)}, bf16[64,512]{1,0:T(8,128)(2,1)S(1)}, u32[]{:S(2)}, u32[]{:S(2)}) collective-permute-start(bf16[64,512]{1,0:T(8,128)(2,1)S(1)} %bitcast.374), channel_id=1, source_target_pairs={{0,16},{8,24},{16,0},{24,8},{1,17},{9,25},{17,1},{25,9},{2,18},{10... | collective-permute-start | bytes 196616 | tf_op jit(solution)/shard_map/ppermute | solution.py:12
  538.5 120.9 %collective-permute-start.10 = (bf16[64,512]{1,0:T(8,128)(2,1)S(1)}, bf16[64,512]{1,0:T(8,128)(2,1)S(1)}, u32[]{:S(2)}, u32[]{:S(2)}) collective-permute-start(bf16[64,512]{1,0:T(8,128)(2,1)S(1)} %bitcast.373), channel_id=1, source_target_pairs={{0,1},{1,0},{2,3},{3,2},{4,5},{5,4},{6,7},{7,6},{8,9},{9,8},{10,11... | collective-permute-start | bytes 196616 | tf_op jit(solution)/shard_map/ppermute | solution.py:12
Sparse Core Ops, SparseCore 0:
  27.5 120.8 all-reduce.4
  185.2 20.8 reduce-scatter.3
  257.3 125.2 all-reduce.6
  458.6 21.9 reduce-scatter.5
  531.8 125.2 all-reduce.8
  733.1 21.9 reduce-scatter.7
where the time goes:
time: 808 us; the launch traced here: 806 us
  waiting for transfers between devices  411 us (51%)
  blocking collectives  291 us (36%)
  matrix products  43.6 us (5%)
  starting transfers between devices  23 us (3%)
  other arithmetic  18.3 us (2%)
  between operations  14.7 us (2%)
    psum x3, waiting for transfers between devices, precondition(): lax.psum((coefficients[level_total - 1], partial_energy), ('hi', 'lo'))  346 us
    psum x3, blocking collectives, precondition(): lax.psum((coefficients[level_total - 1], partial_energy), ('hi', 'lo'))  118 us
    all_gather x3, blocking collectives, local(): lax.all_gather(rounded, 'lo', axis=0, tiled=True)  93.7 us
    psum x2, blocking collectives, local(): curvature = lax.psum(jnp.sum(direction * image, axis=0), ('hi', 'lo'))  78.8 us
    reduce_scatter x3, waiting for transfers between devices, local(): lax.psum_scatter(partial_value, 'hi', scatter_dimension=0, tiled=True)  64.5 us
    ppermute x15, starting transfers between devices, from_partner(): return lax.ppermute(value, axis, pairs)  22.8 us
    dot_general x15, matrix products, level_pieces(): own_part = jnp.einsum('l,lrb->rb', select, coefficients)  20.4 us
  transfers between devices with their start and end apart: 21, of which 6 were waited for; matrix products, arithmetic and copies ran while one was open for 3% of the time, Pallas kernels for 0%

commit v1 on v0

--- a/solution.py
+++ b/solution.py
@@ -84,7 +84,7 @@
         )
         product = lax.psum_scatter(partial_value, "hi", scatter_dimension=0, tiled=True)
         image = genetic * product + noise * direction
-        curvature = lax.psum(jnp.sum(direction * image, axis=0), ("hi", "lo"))
+        curvature = lax.psum(lax.psum(jnp.sum(direction * image, axis=0), "hi"), "lo")
         alpha = energy / curvature
         stepsize = jnp.where(step < iters_per_column, alpha, jnp.zeros_like(alpha))
         solution = solution + stepsize * direction

time: 808 us -> 780 us (0.965)
  waiting for transfers between devices: 411 us -> 392 us
  starting transfers between devices: 23 us -> 14.4 us
    reduce_scatter x3, waiting for transfers between devices: 64.5 us -> 44.1 us  [local(): lax.psum_scatter(partial_value, 'hi', scatter_dimension=0, tiled=True)]
    ppermute x15, starting transfers between devices: 22.8 us -> 14.1 us  [from_partner(): return lax.ppermute(value, axis, pairs)]
    psum x2 -> x6, blocking collectives: 78.8 us -> 80.9 us  [the longest x3 62.7 us: local(): lax.psum(lax.psum(jnp.sum(direction * image, axis=0), 'hi'), 'lo')]
  transfers between devices with their start and end apart: 21 -> 21, of which waited for: 6 -> 5; matrix products, arithmetic and copies ran while one was open for 3% -> 3% of each run, Pallas kernels for 0% -> 0%
where the time goes in v1:
time: 780 us; the launch traced here: 779 us
  waiting for transfers between devices  392 us (50%)
  blocking collectives  291 us (37%)
  matrix products  43.6 us (6%)
  other arithmetic  18.3 us (2%)
  between operations  14.7 us (2%)
  starting transfers between devices  14.4 us (2%)
    psum x3, waiting for transfers between devices, precondition(): lax.psum((coefficients[level_total - 1], partial_energy), ('hi', 'lo'))  348 us
    psum x3, blocking collectives, precondition(): lax.psum((coefficients[level_total - 1], partial_energy), ('hi', 'lo'))  116 us
    all_gather x3, blocking collectives, local(): lax.all_gather(rounded, 'lo', axis=0, tiled=True)  93.7 us
    psum x3, blocking collectives, local(): lax.psum(lax.psum(jnp.sum(direction * image, axis=0), 'hi'), 'lo')  62.7 us
    reduce_scatter x3, waiting for transfers between devices, local(): lax.psum_scatter(partial_value, 'hi', scatter_dimension=0, tiled=True)  44.1 us
    dot_general x15, matrix products, level_pieces(): own_part = jnp.einsum('l,lrb->rb', select, coefficients)  20.4 us
    psum x3, blocking collectives, local(): lax.psum(jnp.sum(direction * image, axis=0), 'hi')  18.2 us
  transfers between devices with their start and end apart: 21, of which 5 were waited for; matrix products, arithmetic and copies ran while one was open for 3% of the time, Pallas kernels for 0%

profile of v1, /device:TPU:0, one launch (start us, length us, event | category | flops | bytes accessed | tf_op | source)
XLA Modules:
  0.0 779.1 jit_solution(11061564961943452731)
XLA Ops:
  7.2 1.5 fusion.146
  8.7 2.1 fusion.150
  10.8 1.3 fusion.26
  12.1 3.1 collective-permute-start.1
  15.3 1.4 fusion.24
  16.6 2.7 collective-permute-start.2
  19.3 1.4 fusion.22
  20.8 1.4 fusion.20
  22.1 1.6 collective-permute-start.4
  23.7 1.4 fusion.28
  25.1 1.6 collective-permute-start
  30.6 0.9 fusion.58
  31.5 0.9 fusion.54
  32.4 0.8 fusion.56
  33.3 0.9 fusion.50
  34.2 0.9 fusion.52
  35.8 112.5 %all-reduce.4.cloned.1.call-done = f32[64,512]{1,0:T(8,128)} async-done(((f32[64,512]{1,0:T(8,128)}), f32[64,512]{1,0:T(8,128)}) %all-reduce.4.cloned.1.call-update) | async-done | bytes 131088 | tf_op jit(solution)/shard_map/psum | solution.py:66
  148.4 1.3 fusion.72
  151.6 0.8 multiply_reduce_fusion.5
  152.7 31.3 %all_gather.9 = bf16[512,512]{1,0:T(8,128)(2,1)S(1)} all-gather(bf16[64,512]{1,0:T(8,128)(2,1)S(1)} %get-tuple-element.17), channel_id=1, replica_groups=mesh['hi'=4,'lo'=8] {'lo'}, dimensions={0}, use_global_device_ids=true | all-gather | bytes 589824 | tf_op jit(solution)/shard_map/all_gather | solution.py:82
  184.0 1.1 convolution_bitcast_fusion.2
  185.8 37.7 %psum.84 = f32[512]{0:T(512)S(1)} all-reduce(f32[512]{0:T(512)S(1)} %get-tuple-element.19), channel_id=1, replica_groups=mesh['hi'=4,'lo'=8] {'hi','lo'}, use_global_device_ids=true, to_apply=%region_1.0 | all-reduce | flops 512 | bytes 4096 | tf_op jit(solution)/shard_map/psum | solution.py:66
  223.4 2.2 multiply_reduce_fusion.4
  225.6 6.7 psum.86
  232.3 19.5 %psum.87 = f32[512]{0:T(512)S(1)} all-reduce(f32[512]{0:T(512)S(1)} %psum.86), channel_id=1, replica_groups=mesh['hi'=4,'lo'=8] {'lo'}, use_global_device_ids=true, to_apply=%region_7.0 | all-reduce | flops 512 | bytes 4096 | tf_op jit(solution)/shard_map/psum | solution.py:87
  251.8 2.2 multiply_subtract_fusion.2
  254.0 1.1 fusion.151
  255.1 1.3 fusion.16
  256.4 1.4 fusion.14
  257.8 1.4 fusion.12
  259.2 1.4 fusion.10
  261.3 1.4 fusion.18
  263.0 1.8 collective-permute-start.9
  264.8 0.9 collective-permute-start.5
  265.7 117.7 %all-reduce.6.cloned.1.call-done = f32[64,512]{1,0:T(8,128)} async-done(((f32[64,512]{1,0:T(8,128)}), f32[64,512]{1,0:T(8,128)}) %all-reduce.6.cloned.1.call-update) | async-done | bytes 131088 | tf_op jit(solution)/shard_map/psum | solution.py:66
  383.4 1.3 fusion.66
  386.6 0.8 multiply_reduce_fusion.3
  387.4 39.2 %psum.88 = f32[512]{0:T(512)S(1)} all-reduce(f32[512]{0:T(512)S(1)} %get-tuple-element.23), channel_id=1, replica_groups=mesh['hi'=4,'lo'=8] {'hi','lo'}, use_global_device_ids=true, to_apply=%region_9.10 | all-reduce | flops 512 | bytes 4096 | tf_op jit(solution)/shard_map/psum | solution.py:66
  426.9 31.2 %all_gather.10 = bf16[512,512]{1,0:T(8,128)(2,1)S(1)} all-gather(bf16[64,512]{1,0:T(8,128)(2,1)S(1)} %get-tuple-element.27), channel_id=1, replica_groups=mesh['hi'=4,'lo'=8] {'lo'}, dimensions={0}, use_global_device_ids=true | all-gather | bytes 589824 | tf_op jit(solution)/shard_map/all_gather | solution.py:82
  458.2 1.1 convolution_bitcast_fusion.1
  459.3 22.0 %reduce-scatter.6.cloned.1.call-done = f32[64,512]{1,0:T(8,128)} async-done(((f32[256,512]{1,0:T(8,128)}), f32[64,512]{1,0:T(8,128)}) %reduce-scatter.6.cloned.1.call-update) | async-done | bytes 131088 | tf_op jit(solution)/shard_map/reduce_scatter | solution.py:85
  481.3 2.2 multiply_reduce_fusion.2
  483.5 5.8 psum.90
  489.2 21.7 %psum.91 = f32[512]{0:T(512)S(1)} all-reduce(f32[512]{0:T(512)S(1)} %psum.90), channel_id=1, replica_groups=mesh['hi'=4,'lo'=8] {'lo'}, use_global_device_ids=true, to_apply=%region_15.16 | all-reduce | flops 512 | bytes 4096 | tf_op jit(solution)/shard_map/psum | solution.py:87
  511.0 2.2 multiply_subtract_fusion.1
  513.2 1.1 fusion.152
  514.3 1.3 fusion.6
  515.6 1.4 fusion.4
  517.0 1.4 fusion.2
  518.3 1.4 fusion
  520.4 1.4 fusion.8
  522.1 1.1 collective-permute-start.14
  523.2 0.9 collective-permute-start.10
  524.1 117.7 %all-reduce.8.cloned.1.call-done = f32[64,512]{1,0:T(8,128)} async-done(((f32[64,512]{1,0:T(8,128)}), f32[64,512]{1,0:T(8,128)}) %all-reduce.8.cloned.1.call-update) | async-done | bytes 131088 | tf_op jit(solution)/shard_map/psum | solution.py:66
  641.9 1.3 fusion.60
  645.0 0.8 multiply_reduce_fusion.1
  645.8 39.3 %psum.92 = f32[512]{0:T(512)S(1)} all-reduce(f32[512]{0:T(512)S(1)} %get-tuple-element.29), channel_id=1, replica_groups=mesh['hi'=4,'lo'=8] {'hi','lo'}, use_global_device_ids=true, to_apply=%region_17.18 | all-reduce | flops 512 | bytes 4096 | tf_op jit(solution)/shard_map/psum | solution.py:66
  685.4 31.2 %all_gather.11 = bf16[512,512]{1,0:T(8,128)(2,1)S(1)} all-gather(bf16[64,512]{1,0:T(8,128)(2,1)S(1)} %get-tuple-element.33), channel_id=1, replica_groups=mesh['hi'=4,'lo'=8] {'lo'}, dimensions={0}, use_global_device_ids=true | all-gather | bytes 589824 | tf_op jit(solution)/shard_map/all_gather | solution.py:82
  716.6 1.1 convolution_bitcast_fusion
  717.8 22.1 %reduce-scatter.8.cloned.1.call-done = f32[64,512]{1,0:T(8,128)} async-done(((f32[256,512]{1,0:T(8,128)}), f32[64,512]{1,0:T(8,128)}) %reduce-scatter.8.cloned.1.call-update) | async-done | bytes 131088 | tf_op jit(solution)/shard_map/reduce_scatter | solution.py:85
  739.9 2.2 multiply_reduce_fusion
  742.1 5.8 psum.94
  747.8 21.5 %psum.95 = f32[512]{0:T(512)S(1)} all-reduce(f32[512]{0:T(512)S(1)} %psum.94), channel_id=1, replica_groups=mesh['hi'=4,'lo'=8] {'lo'}, use_global_device_ids=true, to_apply=%region_23.24 | all-reduce | flops 512 | bytes 4096 | tf_op jit(solution)/shard_map/psum | solution.py:87
  769.3 2.9 multiply_subtract_fusion
  (114 shorter events, 13.8 us)
Async XLA Ops:
  7.2 176.8 %copy-start = (bf16[4,1,64,1,512]{4,2,3,1,0:T(8,128)(2,1)S(1)}, bf16[4,1,64,1,512]{4,2,3,1,0:T(8,128)(2,1)}, u32[]{:S(2)}) copy-start(bf16[4,1,64,1,512]{4,2,3,1,0:T(8,128)(2,1)} %param.8) | copy-start | bytes 786436
  7.2 141.2 %all-reduce.4.cloned.1.call-start = ((), (), s32[]{:S(2)}) async-start(), calls=%async_computation.3 | async-start | bytes 262144 | tf_op jit(solution)/shard_map/psum | solution.py:66
  12.1 137.5 %collective-permute-start.1 = (bf16[64,512]{1,0:T(8,128)(2,1)S(1)}, bf16[64,512]{1,0:T(8,128)(2,1)S(1)}, u32[]{:S(2)}, u32[]{:S(2)}) collective-permute-start(bf16[64,512]{1,0:T(8,128)(2,1)S(1)} %bitcast.372), channel_id=1, source_target_pairs={{0,2},{1,3},{2,0},{3,1},{4,6},{5,7},{6,4},{7,5},{8,10},{9,11},{10,... | collective-permute-start | bytes 196616 | tf_op jit(solution)/shard_map/ppermute | solution.py:12
  16.6 133.3 %collective-permute-start.2 = (bf16[64,512]{1,0:T(8,128)(2,1)S(1)}, bf16[64,512]{1,0:T(8,128)(2,1)S(1)}, u32[]{:S(2)}, u32[]{:S(2)}) collective-permute-start(bf16[64,512]{1,0:T(8,128)(2,1)S(1)} %bitcast.371), channel_id=1, source_target_pairs={{0,4},{1,5},{2,6},{3,7},{4,0},{5,1},{6,2},{7,3},{8,12},{9,13},{10,... | collective-permute-start | bytes 196616 | tf_op jit(solution)/shard_map/ppermute | solution.py:12
  20.7 129.5 %collective-permute-start.3 = (bf16[64,512]{1,0:T(8,128)(2,1)S(1)}, bf16[64,512]{1,0:T(8,128)(2,1)S(1)}, u32[]{:S(2)}, u32[]{:S(2)}) collective-permute-start(bf16[64,512]{1,0:T(8,128)(2,1)S(1)} %bitcast.370), channel_id=1, source_target_pairs={{0,8},{8,0},{16,24},{24,16},{1,9},{9,1},{17,25},{25,17},{2,10},{10... | collective-permute-start | bytes 196616 | tf_op jit(solution)/shard_map/ppermute | solution.py:12
  22.1 8.5 %copy-start.1 = (f32[9,64,64]{2,1,0:T(8,128)S(1)}, f32[9,64,64]{2,1,0:T(8,128)}, u32[]{:S(2)}) copy-start(f32[9,64,64]{2,1,0:T(8,128)} %param.12) | copy-start | bytes 442372
  22.1 128.4 %collective-permute-start.4 = (bf16[64,512]{1,0:T(8,128)(2,1)S(1)}, bf16[64,512]{1,0:T(8,128)(2,1)S(1)}, u32[]{:S(2)}, u32[]{:S(2)}) collective-permute-start(bf16[64,512]{1,0:T(8,128)(2,1)S(1)} %bitcast.368), channel_id=1, source_target_pairs={{0,16},{8,24},{16,0},{24,8},{1,17},{9,25},{17,1},{25,9},{2,18},{10... | collective-permute-start | bytes 196616 | tf_op jit(solution)/shard_map/ppermute | solution.py:12
  25.1 125.7 %collective-permute-start = (bf16[64,512]{1,0:T(8,128)(2,1)S(1)}, bf16[64,512]{1,0:T(8,128)(2,1)S(1)}, u32[]{:S(2)}, u32[]{:S(2)}) collective-permute-start(bf16[64,512]{1,0:T(8,128)(2,1)S(1)} %bitcast.369), channel_id=1, source_target_pairs={{0,1},{1,0},{2,3},{3,2},{4,5},{5,4},{6,7},{7,6},{8,9},{9,8},{10,11... | collective-permute-start | bytes 196616 | tf_op jit(solution)/shard_map/ppermute | solution.py:12
  27.4 196.1 %reduce-scatter.4.cloned.1.call-start = ((), (), s32[]{:S(2)}) async-start(), calls=%async_computation.4 | async-start | bytes 655360 | tf_op jit(solution)/shard_map/reduce_scatter | solution.py:85
  150.5 1.1 copy-start.2
  150.5 1.0 copy-start.3
  150.5 1.0 copy-start.5
  152.7 32.5 %copy-start.6 = (f32[2]{0:T(128)S(1)}, f32[2]{0:T(128)}, u32[]{:S(2)}) copy-start(f32[2]{0:T(128)} %param.14) | copy-start | bytes 28
  184.0 67.8 %copy-start.4 = (s32[512]{0:T(512)S(1)}, s32[512]{0:T(512)}, u32[]{:S(2)}) copy-start(s32[512]{0:T(512)} %param.15) | copy-start | bytes 6148
  185.1 198.3 %all-reduce.6.cloned.1.call-start = ((), (), s32[]{:S(2)}) async-start(), calls=%async_computation.5 | async-start | bytes 262144 | tf_op jit(solution)/shard_map/psum | solution.py:66
  261.2 220.1 %reduce-scatter.6.cloned.1.call-start = ((), (), s32[]{:S(2)}) async-start(), calls=%async_computation.6 | async-start | bytes 655360 | tf_op jit(solution)/shard_map/reduce_scatter | solution.py:85
  262.7 122.0 %collective-permute-start.6 = (bf16[64,512]{1,0:T(8,128)(2,1)S(1)}, bf16[64,512]{1,0:T(8,128)(2,1)S(1)}, u32[]{:S(2)}, u32[]{:S(2)}) collective-permute-start(bf16[64,512]{1,0:T(8,128)(2,1)S(1)} %bitcast.381), channel_id=1, source_target_pairs={{0,2},{1,3},{2,0},{3,1},{4,6},{5,7},{6,4},{7,5},{8,10},{9,11},{10,... | collective-permute-start | bytes 196616 | tf_op jit(solution)/shard_map/ppermute | solution.py:12
  262.8 122.2 %collective-permute-start.7 = (bf16[64,512]{1,0:T(8,128)(2,1)S(1)}, bf16[64,512]{1,0:T(8,128)(2,1)S(1)}, u32[]{:S(2)}, u32[]{:S(2)}) collective-permute-start(bf16[64,512]{1,0:T(8,128)(2,1)S(1)} %bitcast.380), channel_id=1, source_target_pairs={{0,4},{1,5},{2,6},{3,7},{4,0},{5,1},{6,2},{7,3},{8,12},{9,13},{10,... | collective-permute-start | bytes 196616 | tf_op jit(solution)/shard_map/ppermute | solution.py:12
  262.9 122.4 %collective-permute-start.8 = (bf16[64,512]{1,0:T(8,128)(2,1)S(1)}, bf16[64,512]{1,0:T(8,128)(2,1)S(1)}, u32[]{:S(2)}, u32[]{:S(2)}) collective-permute-start(bf16[64,512]{1,0:T(8,128)(2,1)S(1)} %bitcast.378), channel_id=1, source_target_pairs={{0,8},{8,0},{16,24},{24,16},{1,9},{9,1},{17,25},{25,17},{2,10},{10... | collective-permute-start | bytes 196616 | tf_op jit(solution)/shard_map/ppermute | solution.py:12
  263.0 122.6 %collective-permute-start.9 = (bf16[64,512]{1,0:T(8,128)(2,1)S(1)}, bf16[64,512]{1,0:T(8,128)(2,1)S(1)}, u32[]{:S(2)}, u32[]{:S(2)}) collective-permute-start(bf16[64,512]{1,0:T(8,128)(2,1)S(1)} %bitcast.376), channel_id=1, source_target_pairs={{0,16},{8,24},{16,0},{24,8},{1,17},{9,25},{17,1},{25,9},{2,18},{10... | collective-permute-start | bytes 196616 | tf_op jit(solution)/shard_map/ppermute | solution.py:12
  264.8 121.0 %collective-permute-start.5 = (bf16[64,512]{1,0:T(8,128)(2,1)S(1)}, bf16[64,512]{1,0:T(8,128)(2,1)S(1)}, u32[]{:S(2)}, u32[]{:S(2)}) collective-permute-start(bf16[64,512]{1,0:T(8,128)(2,1)S(1)} %bitcast.375), channel_id=1, source_target_pairs={{0,1},{1,0},{2,3},{3,2},{4,5},{5,4},{6,7},{7,6},{8,9},{9,8},{10,11... | collective-permute-start | bytes 196616 | tf_op jit(solution)/shard_map/ppermute | solution.py:12
  459.3 182.6 %all-reduce.8.cloned.1.call-start = ((), (), s32[]{:S(2)}) async-start(), calls=%async_computation.7 | async-start | bytes 262144 | tf_op jit(solution)/shard_map/psum | solution.py:66
  520.4 219.5 %reduce-scatter.8.cloned.1.call-start = ((), (), s32[]{:S(2)}) async-start(), calls=%async_computation.8 | async-start | bytes 655360 | tf_op jit(solution)/shard_map/reduce_scatter | solution.py:85
  521.8 121.3 %collective-permute-start.11 = (bf16[64,512]{1,0:T(8,128)(2,1)S(1)}, bf16[64,512]{1,0:T(8,128)(2,1)S(1)}, u32[]{:S(2)}, u32[]{:S(2)}) collective-permute-start(bf16[64,512]{1,0:T(8,128)(2,1)S(1)} %bitcast.382), channel_id=1, source_target_pairs={{0,2},{1,3},{2,0},{3,1},{4,6},{5,7},{6,4},{7,5},{8,10},{9,11},{10,... | collective-permute-start | bytes 196616 | tf_op jit(solution)/shard_map/ppermute | solution.py:12
  521.9 121.5 %collective-permute-start.12 = (bf16[64,512]{1,0:T(8,128)(2,1)S(1)}, bf16[64,512]{1,0:T(8,128)(2,1)S(1)}, u32[]{:S(2)}, u32[]{:S(2)}) collective-permute-start(bf16[64,512]{1,0:T(8,128)(2,1)S(1)} %bitcast.379), channel_id=1, source_target_pairs={{0,4},{1,5},{2,6},{3,7},{4,0},{5,1},{6,2},{7,3},{8,12},{9,13},{10,... | collective-permute-start | bytes 196616 | tf_op jit(solution)/shard_map/ppermute | solution.py:12
  522.0 121.7 %collective-permute-start.13 = (bf16[64,512]{1,0:T(8,128)(2,1)S(1)}, bf16[64,512]{1,0:T(8,128)(2,1)S(1)}, u32[]{:S(2)}, u32[]{:S(2)}) collective-permute-start(bf16[64,512]{1,0:T(8,128)(2,1)S(1)} %bitcast.377), channel_id=1, source_target_pairs={{0,8},{8,0},{16,24},{24,16},{1,9},{9,1},{17,25},{25,17},{2,10},{10... | collective-permute-start | bytes 196616 | tf_op jit(solution)/shard_map/ppermute | solution.py:12
  522.1 121.9 %collective-permute-start.14 = (bf16[64,512]{1,0:T(8,128)(2,1)S(1)}, bf16[64,512]{1,0:T(8,128)(2,1)S(1)}, u32[]{:S(2)}, u32[]{:S(2)}) collective-permute-start(bf16[64,512]{1,0:T(8,128)(2,1)S(1)} %bitcast.374), channel_id=1, source_target_pairs={{0,16},{8,24},{16,0},{24,8},{1,17},{9,25},{17,1},{25,9},{2,18},{10... | collective-permute-start | bytes 196616 | tf_op jit(solution)/shard_map/ppermute | solution.py:12
  523.2 121.0 %collective-permute-start.10 = (bf16[64,512]{1,0:T(8,128)(2,1)S(1)}, bf16[64,512]{1,0:T(8,128)(2,1)S(1)}, u32[]{:S(2)}, u32[]{:S(2)}) collective-permute-start(bf16[64,512]{1,0:T(8,128)(2,1)S(1)} %bitcast.373), channel_id=1, source_target_pairs={{0,1},{1,0},{2,3},{3,2},{4,5},{5,4},{6,7},{7,6},{8,9},{9,8},{10,11... | collective-permute-start | bytes 196616 | tf_op jit(solution)/shard_map/ppermute | solution.py:12
Sparse Core Ops, SparseCore 0:
  27.5 120.8 all-reduce.3
  185.2 20.8 reduce-scatter.3
  261.3 122.0 all-reduce.5
  459.4 21.8 reduce-scatter.5
  520.5 121.3 all-reduce.7
  717.9 21.9 reduce-scatter.7
